TPU v7x, 32 devices: a whole 2x2x4 slice. The times are simulated.
32 devices in a mesh: rep: 4 (over z), fsdp: 2 (over x), tp: 4 (over y, core).
Axes of the slice: x: 2, y: 2, z: 4, core: 2. Of those that a mesh axis runs over, the one named last changes fastest.
Arguments:
- gate_pre: bfloat16 [1024, 14848], P(('rep', 'fsdp'), 'tp'), may hold values from -6 to 6
- up_pre: bfloat16 [1024, 14848], P(('rep', 'fsdp'), 'tp'), may hold values from -30 to 30
- out_grad: bfloat16 [1024, 4096], P(('rep', 'fsdp')), may hold values from -30 to 30
Outputs:
- down_grad: bfloat16 [4096, 14848], P('fsdp', 'tp')
All inputs are finite; a program needn't handle non-finite values.
Results may differ from a plain program's by a relative error of at most 0.02.
Values may be sent and summed in bfloat16 or wider, within the bound.
A program may use at most 128 MiB of HBM per device.

v0:
```python
import jax
import jax.numpy as jnp
from jax import lax
from jax.sharding import PartitionSpec as P


def on_device(gate_pre, up_pre, out_grad):
    hidden = (jax.nn.silu(gate_pre.astype(jnp.float32)) * up_pre.astype(jnp.float32)).astype(
        jnp.bfloat16
    )
    feature_rows = out_grad.shape[1] // lax.axis_size("fsdp")
    block_rows = out_grad.shape[0]
    spread = lax.all_to_all(out_grad, "fsdp", split_axis=1, concat_axis=0, tiled=True)

    def advance(running, paired):
        grad_rows, hidden_rows = paired
        partial_term = jnp.dot(grad_rows.T, hidden_rows, preferred_element_type=jnp.float32)
        return (running + partial_term.astype(jnp.bfloat16).astype(jnp.float32), None)

    starting = jnp.zeros((feature_rows, hidden.shape[1]), jnp.float32)
    running = starting
    portion = lax.all_gather(hidden, "fsdp", axis=0, tiled=True)
    row_count = portion.shape[0]
    blocks = row_count // block_rows
    grad_rows = spread
    running, unused = lax.scan(
        advance,
        running,
        (
            grad_rows.reshape(blocks, block_rows, grad_rows.shape[1]),
            portion.reshape(blocks, block_rows, portion.shape[1]),
        ),
    )
    summed = lax.psum(running.astype(jnp.bfloat16), "rep").astype(jnp.float32)
    square_total = lax.psum(jnp.sum(summed * summed), ("fsdp", "tp"))
    entry_count = summed.shape[0] * lax.axis_size("fsdp") * summed.shape[1] * lax.axis_size("tp")
    factor = 1.0 / jnp.sqrt(square_total / entry_count + 1e-06)
    return (summed * factor).astype(jnp.bfloat16)


def solution(mesh):
    return jax.shard_map(
        on_device,
        mesh=mesh,
        in_specs=(P(("rep", "fsdp"), "tp"), P(("rep", "fsdp"), "tp"), P(("rep", "fsdp"), None)),
        out_specs=P("fsdp", "tp"),
        check_vma=False,
    )
```

profile of v0, /device:TPU:0, one launch (start us, length us, event | category | flops | bytes accessed | tf_op | source)
XLA Modules:
  0.0 660.7 jit_solution(3080684873038719467)
XLA Ops:
  6.5 0.0 all-gather.2.cloned.1.call-start
  6.5 3.0 fusion.11
  9.5 0.0 all-gather.2.cloned.1.call-update
  9.6 2.3 copy.4
  11.8 4.2 all-to-all-start
  16.1 0.0 all-reduce.2.cloned.1.call-start
  16.1 23.0 %all-to-all-done = bf16[128,2,2048]{0,2,1:T(8,128)(2,1)S(1)} async-done(((bf16[128,2,2048]{0,2,1:T(8,128)(2,1)}), bf16[128,2,2048]{0,2,1:T(8,128)(2,1)S(1)}, u32[]{:S(2)}, u32[]{:S(2)}) %all-to-all-start) | async-done | bytes 1048608 | tf_op jit(solution)/shard_map/all_to_all | solution.py:13
  39.1 12.0 %all-gather.2.cloned.1.call-done = bf16[256,3712]{1,0:T(8,128)(2,1)} async-done(((bf16[128,3712]{1,0:T(8,128)(2,1)}), bf16[256,3712]{1,0:T(8,128)(2,1)}) %all-gather.2.cloned.1.call-update) | async-done | bytes 1900560 | tf_op jit(solution)/shard_map/all_gather | solution.py:22
  51.1 35.5 %while.11 = (s32[]{:T(128)}, f32[2048,3712]{1,0:T(8,128)}, bf16[2,128,2048]{1,2,0:T(8,128)(2,1)S(1)}, bf16[2,128,3712]{2,1,0:T(8,128)(2,1)}, s32[]{:T(128)}, /*index=5*/s32[]{:T(128)}) while((s32[]{:T(128)}, f32[2048,3712]{1,0:T(8,128)}, bf16[2,128,2048]{1,2,0:T(8,128)(2,1)S(1)}, bf16[2,128,3712]{2,1,0:T(8,128)(2,1)}, s32[]{:T(128)}, ...), condition=%wide.region_1.2_spmd.clone, body=%wide.region_0.1_spmd.clone.sunk | while | flops 1976565760 | bytes 62293588 | solution.py:26
  51.1 12.6 %select_add_fusion.2 = f32[2048,3712]{1,0:T(8,128)} fusion(f32[2048,3712]{1,0:T(8,128)} %get-tuple-element.87, pred[]{:T(512)S(6)} %compare.3, bf16[2,128,3712]{2,1,0:T(8,128)(2,1)} %get-tuple-element.95, s32[]{:T(128)S(6)} %copy.9, bf16[2,128,2048]{1,2,0:T(8,128)(2,1)S(1)} %get-tuple-element.94), kind=kOutput, calls=%fused_computation.clone.1 | convolution fusion | flops 1976565760 | bytes 62293504 | tf_op jit(solution)/shard_map/while/body/eval_jaxpr/dot_general | solution.py:17
  63.7 22.9 %select_add_fusion.2 = f32[2048,3712]{1,0:T(8,128)} fusion(f32[2048,3712]{1,0:T(8,128)} %get-tuple-element.87, pred[]{:T(512)S(6)} %compare.3, bf16[2,128,3712]{2,1,0:T(8,128)(2,1)} %get-tuple-element.95, s32[]{:T(128)S(6)} %copy.9, bf16[2,128,2048]{1,2,0:T(8,128)(2,1)S(1)} %get-tuple-element.94), kind=kOutput, calls=%fused_computation.clone.1 | convolution fusion | flops 1976565760 | bytes 62293504 | tf_op jit(solution)/shard_map/while/body/eval_jaxpr/dot_general | solution.py:17
  86.6 15.9 %convert_element_type.27 = bf16[2048,3712]{1,0:T(8,128)(2,1)} convert(f32[2048,3712]{1,0:T(8,128)} %get-tuple-element.27) | non-fusion elementwise | flops 7602176 | bytes 45613056 | tf_op jit(solution)/shard_map/convert_element_type | solution.py:34
  102.5 0.0 all-reduce.2.cloned.1.call-update
  102.6 511.4 %all-reduce.2.cloned.1.call-done = bf16[2048,3712]{1,0:T(8,128)(2,1)} async-done(((bf16[2048,3712]{1,0:T(8,128)(2,1)}), bf16[2048,3712]{1,0:T(8,128)(2,1)}) %all-reduce.2.cloned.1.call-update) | async-done | bytes 15204368 | tf_op jit(solution)/shard_map/psum | solution.py:34
  614.0 13.7 %fusion.5 = f32[]{:T(128)} fusion(bf16[2048,3712]{1,0:T(8,128)(2,1)} %all-reduce.2.cloned.1.call-done), kind=kLoop, calls=%fused_computation.8 | loop fusion | flops 22806528 | bytes 15204356 | tf_op jit(solution)/shard_map/reduce_sum | solution.py:35
  627.7 14.1 %psum.15 = f32[]{:T(128)} all-reduce(f32[]{:T(128)} %fusion.5), channel_id=1, replica_groups=mesh['rep'=4,'fsdp'=2,'tp'=4] {'fsdp','tp'}, use_global_device_ids=true, to_apply=%region_4.5 | all-reduce | flops 1 | bytes 8 | tf_op jit(solution)/shard_map/psum | solution.py:35
  642.5 11.4 %fusion.6 = bf16[2048,3712]{1,0:T(8,128)(2,1)} fusion(bf16[2048,3712]{1,0:T(8,128)(2,1)} %all-reduce.2.cloned.1.call-done, f32[]{:T(128)S(6)} %sqrt.3), kind=kLoop, calls=%fused_computation.9 | loop fusion | flops 22806528 | bytes 30408708 | tf_op jit(solution)/shard_map/convert_element_type | solution.py:38
  (1 shorter events, 0.0 us)
Async XLA Ops:
  6.5 44.6 %all-gather.2.cloned.1.call-start = ((), (), s32[]{:S(2)}) async-start(), calls=%async_computation.1 | async-start | bytes 2850816 | tf_op jit(solution)/shard_map/all_gather | solution.py:22
  11.8 27.3 %all-to-all-start = ((bf16[128,2,2048]{0,2,1:T(8,128)(2,1)}), bf16[128,2,2048]{0,2,1:T(8,128)(2,1)S(1)}, u32[]{:S(2)}, u32[]{:S(2)}) async-start(bf16[128,2,2048]{0,2,1:T(8,128)(2,1)} %bitcast), calls=%async_computation | async-start | bytes 2097152 | tf_op jit(solution)/shard_map/all_to_all | solution.py:13
  16.1 597.9 %all-reduce.2.cloned.1.call-start = ((), (), s32[]{:S(2)}) async-start(), calls=%async_computation.2 | async-start | bytes 30408704 | tf_op jit(solution)/shard_map/psum | solution.py:34
Sparse Core Ops, SparseCore 0:
  9.7 41.3 all-gather.1
  102.7 511.2 all-reduce.1
where the time goes:
time: 661 us
  waiting for transfers between devices  546 us (83%)
  other arithmetic  44.1 us (7%)
  matrix products  35.5 us (5%)
  blocking collectives  14.1 us (2%)
  between operations  14.1 us (2%)
    psum x1, waiting for transfers between devices, on_device(): summed = lax.psum(running.astype(jnp.bfloat16), 'rep').astype(jnp.float32)  511 us
    dot_general x2, matrix products, advance(): jnp.dot(grad_rows.T, hidden_rows, preferred_element_type=jnp.float32)  35.5 us
    all_to_all x1, waiting for transfers between devices, on_device(): lax.all_to_all(out_grad, 'fsdp', split_axis=1, concat_axis=0, tiled=True)  23 us
    convert_element_type x1, other arithmetic, on_device(): summed = lax.psum(running.astype(jnp.bfloat16), 'rep').astype(jnp.float32)  15.9 us
    psum x1, blocking collectives, on_device(): square_total = lax.psum(jnp.sum(summed * summed), ('fsdp', 'tp'))  14.1 us
    reduce_sum x1, other arithmetic, on_device(): square_total = lax.psum(jnp.sum(summed * summed), ('fsdp', 'tp'))  13.7 us
  transfers between devices with their start and end apart: 3, of which 3 were waited for; matrix products, arithmetic and copies ran while one was open for 0% of the time, Pallas kernels for 0%

commit v1 on v0

v1 whole, which is shorter than its diff:
```python
import jax
import jax.numpy as jnp
from jax import lax
from jax.sharding import PartitionSpec as P


def on_device(gate_pre, up_pre, out_grad):
    hidden = (jax.nn.silu(gate_pre.astype(jnp.float32)) * up_pre.astype(jnp.float32)).astype(
        jnp.bfloat16
    )
    spread = lax.all_to_all(out_grad, "fsdp", split_axis=1, concat_axis=0, tiled=True)
    grad_rows = lax.all_gather(spread, "rep", axis=0, tiled=True)
    hidden_rows = lax.all_gather(hidden, ("rep", "fsdp"), axis=0, tiled=True)
    summed = lax.dot_general(
        grad_rows, hidden_rows, (((0,), (0,)), ((), ())), preferred_element_type=jnp.float32
    )
    square_total = lax.psum(jnp.sum(summed * summed), ("fsdp", "tp"))
    entry_count = summed.shape[0] * lax.axis_size("fsdp") * summed.shape[1] * lax.axis_size("tp")
    factor = 1.0 / jnp.sqrt(square_total / entry_count + 1e-06)
    return (summed * factor).astype(jnp.bfloat16)


def solution(mesh):
    return jax.shard_map(
        on_device,
        mesh=mesh,
        in_specs=(P(("rep", "fsdp"), "tp"), P(("rep", "fsdp"), "tp"), P(("rep", "fsdp"), None)),
        out_specs=P("fsdp", "tp"),
        check_vma=False,
    )
```

time: 661 us -> 309 us (0.47)
  waiting for transfers between devices: 546 us -> 194 us
  other arithmetic: 44.1 us -> 19.4 us
  local copies, waits for them, and re-layouts: 2.26 us -> 22 us
  blocking collectives: 14.1 us -> 30.1 us
  matrix products: 35.5 us -> 28.3 us
    psum x1 -> x0, waiting for transfers between devices: 511 us -> none  [on_device(): summed = lax.psum(running.astype(jnp.bfloat16), 'rep').astype(jnp.float32)]
    all_gather x1 -> x2, waiting for transfers between devices: 12 us -> 194 us  [the longest x1 115 us: on_device(): hidden_rows = lax.all_gather(hidden, ('rep', 'fsdp'), axis=0, tiled=True)]
    all_to_all x1 -> x0, waiting for transfers between devices: 23 us -> none  [on_device(): lax.all_to_all(out_grad, 'fsdp', split_axis=1, concat_axis=0, tiled=True)]
    convert_element_type x0 -> x1, local copies, waits for them, and re-layouts: none -> 19 us  [on_device(): return (summed * factor).astype(jnp.bfloat16)]
    all_to_all x0 -> x1, blocking collectives: none -> 17.6 us  [on_device(): lax.all_to_all(out_grad, 'fsdp', split_axis=1, concat_axis=0, tiled=True)]
    convert_element_type x1 -> x0, other arithmetic: 15.9 us -> none  [on_device(): summed = lax.psum(running.astype(jnp.bfloat16), 'rep').astype(jnp.float32)]
    reduce_sum x1 -> x0, other arithmetic: 13.7 us -> none  [on_device(): square_total = lax.psum(jnp.sum(summed * summed), ('fsdp', 'tp'))]
    dot_general x2 -> x1, matrix products: 35.5 us -> 28.3 us  [on_device(): lax.dot_general(grad_rows, hidden_rows, (((0,), (0,)), ((), ())), preferr...]
  transfers between devices with their start and end apart: 3 -> 2, of which waited for: 3 -> 2; matrix products, arithmetic and copies ran while one was open for 0% -> 1% of each run, Pallas kernels for 0% -> 0%
where the time goes in v1:
time: 309 us; the launch traced here: 308 us
  waiting for transfers between devices  194 us (63%)
  blocking collectives  30.1 us (10%)
  matrix products  28.3 us (9%)
  local copies, waits for them, and re-layouts  22 us (7%)
  other arithmetic  19.4 us (6%)
  between operations  14.1 us (5%)
    all_gather x1, waiting for transfers between devices, on_device(): hidden_rows = lax.all_gather(hidden, ('rep', 'fsdp'), axis=0, tiled=True)  115 us
    all_gather x1, waiting for transfers between devices, on_device(): grad_rows = lax.all_gather(spread, 'rep', axis=0, tiled=True)  78.6 us
    dot_general x1, matrix products, on_device(): lax.dot_general(grad_rows, hidden_rows, (((0,), (0,)), ((), ())), preferr...  28.3 us
    convert_element_type x1, local copies, waits for them, and re-layouts, on_device(): return (summed * factor).astype(jnp.bfloat16)  19 us
    all_to_all x1, blocking collectives, on_device(): lax.all_to_all(out_grad, 'fsdp', split_axis=1, concat_axis=0, tiled=True)  17.6 us
    convert_element_type x1, other arithmetic, on_device(): return (summed * factor).astype(jnp.bfloat16)  16.7 us
    psum x1, blocking collectives, on_device(): square_total = lax.psum(jnp.sum(summed * summed), ('fsdp', 'tp'))  12.4 us
  transfers between devices with their start and end apart: 2, of which 2 were waited for; matrix products, arithmetic and copies ran while one was open for 1% of the time, Pallas kernels for 0%

profile of v1, /device:TPU:0, one launch (start us, length us, event | category | flops | bytes accessed | tf_op | source)
XLA Modules:
  0.0 307.9 jit_solution(16072461343263493116)
XLA Ops:
  6.5 0.0 copy-start
  6.5 0.0 all-gather.5.cloned.1.call-start
  6.5 1.7 copy.6
  8.2 17.6 %all_to_all.19 = bf16[128,2,2048]{0,2,1:T(8,128)(2,1)S(1)} all-to-all(bf16[128,2,2048]{0,2,1:T(8,128)(2,1)S(1)} %bitcast.9), channel_id=1, replica_groups=mesh['rep'=4,'fsdp'=2,'tp'=4] {'fsdp'}, dimensions={1} | all-to-all | bytes 2097152 | tf_op jit(solution)/shard_map/all_to_all | solution.py:11
  25.9 1.3 copy.7
  27.2 0.0 all-gather.5.cloned.1.call-update
  27.2 0.0 all-gather.3.cloned.1.call-start
  27.2 0.0 copy-done
  27.3 2.7 fusion.5
  30.0 0.0 all-gather.3.cloned.1.call-update
  30.0 78.6 %all-gather.5.cloned.1.call-done = bf16[1024,2048]{1,0:T(8,128)(2,1)} async-done(((bf16[256,2048]{1,0:T(8,128)(2,1)}), bf16[1024,2048]{1,0:T(8,128)(2,1)}) %all-gather.5.cloned.1.call-update) | async-done | bytes 4194320 | tf_op jit(solution)/shard_map/all_gather | solution.py:12
  108.6 115.4 %all-gather.3.cloned.1.call-done = bf16[1024,3712]{1,0:T(8,128)(2,1)} async-done(((bf16[128,3712]{1,0:T(8,128)(2,1)}), bf16[1024,3712]{1,0:T(8,128)(2,1)}) %all-gather.3.cloned.1.call-update) | async-done | bytes 7602192 | tf_op jit(solution)/shard_map/all_gather | solution.py:13
  224.0 28.3 %multiply_reduce_fusion = (f32[]{:T(128)}, f32[3712,2048]{1,0:T(8,128)}) fusion(bf16[1024,3712]{1,0:T(8,128)(2,1)} %all-gather.3.cloned.1.call-done, bf16[1024,2048]{1,0:T(8,128)(2,1)} %all-gather.5.cloned.1.call-done), kind=kOutput, calls=%fused_computation.1 | convolution fusion | flops 15584460800 | bytes 42205188 | tf_op jit(solution)/shard_map/dot_general | solution.py:14
  252.3 12.4 %psum.7 = f32[]{:T(128)} all-reduce(f32[]{:T(128)} %get-tuple-element.5), channel_id=1, replica_groups=mesh['rep'=4,'fsdp'=2,'tp'=4] {'fsdp','tp'}, use_global_device_ids=true, to_apply=%region_1.2 | all-reduce | flops 1 | bytes 8 | tf_op jit(solution)/shard_map/psum | solution.py:17
  265.4 16.7 %fusion = bf16[2048,3712]{0,1:T(8,128)(2,1)} fusion(f32[3712,2048]{1,0:T(8,128)} %get-tuple-element.6, f32[]{:T(128)S(6)} %sqrt.3), kind=kLoop, calls=%fused_computation.2 | loop fusion | flops 15204352 | bytes 45613060 | tf_op jit(solution)/shard_map/convert_element_type | solution.py:20
  282.1 19.0 %copy.8 = bf16[2048,3712]{1,0:T(8,128)(2,1)} copy(bf16[2048,3712]{0,1:T(8,128)(2,1)} %fusion) | data formatting | bytes 30408704 | tf_op jit(solution)/shard_map/convert_element_type | solution.py:20
Async XLA Ops:
  6.5 20.7 %copy-start = (bf16[128,3712]{1,0:T(8,128)(2,1)S(1)}, bf16[128,3712]{1,0:T(8,128)(2,1)}, u32[]{:S(2)}) copy-start(bf16[128,3712]{1,0:T(8,128)(2,1)} %param.4) | copy-start | bytes 2850820
  6.5 102.1 %all-gather.5.cloned.1.call-start = ((), (), s32[]{:S(2)}) async-start(), calls=%async_computation.2 | async-start | bytes 5242880 | tf_op jit(solution)/shard_map/all_gather | solution.py:12
  27.2 196.8 %all-gather.3.cloned.1.call-start = ((), (), s32[]{:S(2)}) async-start(), calls=%async_computation.1 | async-start | bytes 8552448 | tf_op jit(solution)/shard_map/all_gather | solution.py:13
Sparse Core Ops, SparseCore 0:
  27.3 81.2 all-gather.4
  110.8 113.1 all-gather.2

commit v2 on v1

v2 whole, which is shorter than its diff:
```python
import functools

import jax
import jax.numpy as jnp
from jax import lax
from jax.experimental import pallas as pl
from jax.experimental.pallas import tpu as pltpu
from jax.sharding import PartitionSpec as P

MESH = pl.DeviceIdType.MESH
LANES = 128
VMEM_LIMIT = 60 * 1024 * 1024


def column_chunks(columns):
    chunks, start = [], 0
    for tiles in (6, 4, 2, 1):
        while columns - start >= tiles * LANES:
            chunks.append((start, tiles * LANES))
            start += tiles * LANES
    return chunks


def gather_multiply(
    n_rep, n_tp, hidden_ref, grad_ref, out_ref, square_ref,
    held, grads, turned, staged,
    local_sem, gx_send, gx_recv, gz_send, gz_recv, gt_send, gt_recv,
    hz_send, hz_recv, hx_send, hx_recv, out_sem,
):
    rep = lax.axis_index("rep")
    fsdp = lax.axis_index("fsdp")
    tp = lax.axis_index("tp")
    rows, columns = hidden_ref.shape
    half = grads.shape[1]
    quarter = half // n_tp
    chunks = column_chunks(columns)
    pair = 2 * rows
    my_slot = rep * 2 + fsdp
    my_rows = pl.ds(pl.multiple_of(my_slot * rows, rows), rows)
    other_rows = pl.ds(pl.multiple_of((rep * 2 + 1 - fsdp) * rows, rows), rows)
    across = {"fsdp": 1 - fsdp}
    my_quarter = pl.ds(pl.multiple_of(tp * quarter, LANES), quarter)
    steps = (1, -1)

    def within(at):
        return jnp.logical_and(at >= 0, at < n_rep)

    def block_rows(at, side):
        return pl.ds(pl.multiple_of((at * 2 + side) * rows, rows), rows)

    def pair_rows(at):
        return pl.ds(pl.multiple_of(at * pair, pair), pair)

    barrier = pltpu.get_barrier_semaphore()
    pl.semaphore_signal(barrier, inc=1, device_id=across, device_id_type=MESH)
    for k in range(1, n_tp):
        pl.semaphore_signal(
            barrier, inc=1, device_id={"tp": lax.rem(tp + k, n_tp)}, device_id_type=MESH
        )
    for step in steps:
        @pl.when(within(rep + step))
        def _():
            pl.semaphore_signal(
                barrier, inc=1, device_id={"rep": rep + step}, device_id_type=MESH
            )
    along = jnp.where(rep > 0, 1, 0) + jnp.where(rep < n_rep - 1, 1, 0)
    pl.semaphore_wait(barrier, n_tp + along)

    def remote(src, dst, send, recv, device):
        return pltpu.make_async_remote_copy(
            src_ref=src, dst_ref=dst, send_sem=send, recv_sem=recv,
            device_id=device, device_id_type=MESH,
        )

    def grad_across():
        src = grad_ref.at[:, pl.ds(pl.multiple_of((1 - fsdp) * half + tp * quarter, LANES), quarter)]
        return remote(src, grads.at[my_rows, my_quarter], gx_send, gx_recv, across)

    def grad_hop(i, d):
        spot = grads.at[pair_rows(rep - steps[i] * d), my_quarter]
        return remote(spot, spot, gz_send.at[i, d], gz_recv.at[i, d], {"rep": rep + steps[i]})

    def grad_arrived(i, d):
        spot = grads.at[pair_rows(rep - steps[i] * d), my_quarter]
        return remote(spot, spot, gz_send.at[i, d - 1], gz_recv.at[i, d - 1], {"rep": rep - steps[i]})

    def place(i, d):
        return 0 if d == 0 else 1 + 2 * (d - 1) + i

    def share(i, d, k, towards):
        at = rep - steps[i] * d
        peer = lax.rem(tp + (k if towards else n_tp - k), n_tp)
        source = tp if towards else peer
        cols = pl.ds(pl.multiple_of(source * quarter, LANES), quarter)
        spot = grads.at[other_rows if d == 0 else pair_rows(at), cols]
        return remote(spot, spot, gt_send.at[place(i, d), k - 1], gt_recv.at[place(i, d), k - 1], {"tp": peer})

    def hidden_hop(i, d, c):
        start, size = chunks[c]
        cols = pl.ds(start, size)
        spot = held.at[block_rows(rep - steps[i] * d, fsdp), cols]
        src = hidden_ref.at[:, cols] if d == 0 else spot
        return remote(src, spot, hz_send.at[i, d, c], hz_recv.at[i, d, c], {"rep": rep + steps[i]})

    def hidden_arrived(i, d, c):
        start, size = chunks[c]
        spot = held.at[block_rows(rep - steps[i] * d, fsdp), pl.ds(start, size)]
        return remote(spot, spot, hz_send.at[i, d - 1, c], hz_recv.at[i, d - 1, c], {"rep": rep - steps[i]})

    def hidden_across(i, d, c):
        start, size = chunks[c]
        cols = pl.ds(start, size)
        spot = held.at[block_rows(rep - steps[i] * d, fsdp), cols]
        src = hidden_ref.at[:, cols] if d == 0 else spot
        q = place(i, d)
        return remote(src, spot, hx_send.at[q, c], hx_recv.at[q, c], across)

    def hidden_crossed(i, d, c):
        start, size = chunks[c]
        spot = held.at[block_rows(rep - steps[i] * d, 1 - fsdp), pl.ds(start, size)]
        q = place(i, d)
        return remote(spot, spot, hx_send.at[q, c], hx_recv.at[q, c], across)

    def if_sends(i, act):
        pl.when(within(rep + steps[i]))(act)

    def if_meets(i, d, act):
        pl.when(within(rep - steps[i] * d))(act)

    def if_forwards(i, d, act):
        pl.when(jnp.logical_and(within(rep - steps[i] * d), within(rep + steps[i])))(act)

    count = len(chunks)
    grad_across().start()
    local_grad = pltpu.make_async_copy(
        grad_ref.at[:, pl.ds(pl.multiple_of(fsdp * half, LANES), half)], grads.at[my_rows, :], local_sem.at[0]
    )
    local_hidden = pltpu.make_async_copy(hidden_ref, held.at[my_rows, :], local_sem.at[1])
    local_grad.start()
    local_hidden.start()

    def send_own(c):
        for i in range(2):
            if_sends(i, lambda: hidden_hop(i, 0, c).start())
        hidden_across(0, 0, c).start()

    send_own(0)
    local_grad.wait()
    grad_across().wait_recv()
    for i in range(2):
        if_sends(i, lambda: grad_hop(i, 0).start())
    for k in range(1, n_tp):
        share(0, 0, k, True).start()
    for c in range(1, count):
        send_own(c)

    def take_grad(i, d):
        if_meets(i, d, lambda: grad_arrived(i, d).wait_recv())
        if d < n_rep - 1:
            if_forwards(i, d, lambda: grad_hop(i, d).start())

        def spread():
            for k in range(1, n_tp):
                share(i, d, k, True).start()
        if_meets(i, d, spread)

    def take_hidden(i, d, c):
        if_meets(i, d, lambda: hidden_arrived(i, d, c).wait_recv())
        if d < n_rep - 1:
            if_forwards(i, d, lambda: hidden_hop(i, d, c).start())
        if_meets(i, d, lambda: hidden_across(i, d, c).start())

    for d in range(1, n_rep):
        for i in range(2):
            take_grad(i, d)
        if d < n_rep - 1:
            for c in range(count):
                for i in range(2):
                    take_hidden(i, d, c)

    for k in range(1, n_tp):
        share(0, 0, k, False).wait_recv()
    for d in range(1, n_rep):
        for i in range(2):
            def wait_shared():
                for k in range(1, n_tp):
                    share(i, d, k, False).wait_recv()
            if_meets(i, d, wait_shared)
    tile = 256

    @pl.loop(0, half // tile)
    def _(m):
        spot = pl.ds(pl.multiple_of(m * tile, tile), tile)
        turned[spot, :] = grads[:, spot].T

    local_hidden.wait()
    square_ref[...] = jnp.zeros_like(square_ref)

    def out_copy(c):
        cols = pl.ds(chunks[c][0], chunks[c][1])
        return pltpu.make_async_copy(staged.at[:, cols], out_ref.at[:, cols], out_sem.at[c])

    def multiply(c):
        start, size = chunks[c]
        cols = pl.ds(start, size)
        hidden_crossed(0, 0, c).wait_recv()
        for d in range(1, n_rep):
            for i in range(2):
                if_meets(i, d, lambda: hidden_crossed(i, d, c).wait_recv())

        @pl.loop(0, half // tile)
        def _(m):
            spot = pl.ds(pl.multiple_of(m * tile, tile), tile)
            product = jnp.dot(turned[spot, :], held[:, cols], preferred_element_type=jnp.float32)
            staged[spot, cols] = product.astype(staged.dtype)
            squares = jnp.sum((product * product).reshape(tile // 8, 8, size), axis=0)
            total = squares[:, :LANES]
            for at in range(LANES, size, LANES):
                total = total + squares[:, at:at + LANES]
            square_ref[...] += total

        out_copy(c).start()

    for c in range(count):
        for i in range(2):
            take_hidden(i, n_rep - 1, c)
        if c:
            multiply(c - 1)
    multiply(count - 1)

    grad_across().wait_send()
    for k in range(1, n_tp):
        share(0, 0, k, True).wait_send()
    for i in range(2):
        def sent_own():
            grad_hop(i, 0).wait_send()
            for c in range(count):
                hidden_hop(i, 0, c).wait_send()
        if_sends(i, sent_own)
    for c in range(count):
        hidden_across(0, 0, c).wait_send()
    for d in range(1, n_rep):
        for i in range(2):
            def sent_met():
                for k in range(1, n_tp):
                    share(i, d, k, True).wait_send()
                for c in range(count):
                    hidden_across(i, d, c).wait_send()
            if_meets(i, d, sent_met)
            if d < n_rep - 1:
                def sent_on():
                    grad_hop(i, d).wait_send()
                    for c in range(count):
                        hidden_hop(i, d, c).wait_send()
                if_forwards(i, d, sent_on)
    for c in range(count):
        out_copy(c).wait()


def by_kernel(n_rep, n_tp, hidden, out_grad):
    rows, columns = hidden.shape
    tokens = rows * n_rep * 2
    half = out_grad.shape[1] // 2
    count = len(column_chunks(columns))
    dma = pltpu.SemaphoreType.DMA
    places = 1 + 2 * (n_rep - 1)
    return pl.pallas_call(
        functools.partial(gather_multiply, n_rep, n_tp),
        out_shape=(
            jax.ShapeDtypeStruct((half, columns), jnp.bfloat16),
            jax.ShapeDtypeStruct((8, LANES), jnp.float32),
        ),
        in_specs=[pl.BlockSpec(memory_space=pl.ANY)] * 2,
        out_specs=(pl.BlockSpec(memory_space=pl.ANY), pl.BlockSpec(memory_space=pltpu.VMEM)),
        scratch_shapes=[
            pltpu.VMEM((tokens, columns), jnp.bfloat16),
            pltpu.VMEM((tokens, half), jnp.bfloat16),
            pltpu.VMEM((half, tokens), jnp.bfloat16),
            pltpu.VMEM((half, columns), jnp.bfloat16),
            dma((2,)), dma, dma,
            dma((2, n_rep - 1)), dma((2, n_rep - 1)),
            dma((places, n_tp - 1)), dma((places, n_tp - 1)),
            dma((2, n_rep - 1, count)), dma((2, n_rep - 1, count)),
            dma((places, count)), dma((places, count)),
            dma((count,)),
        ],
        compiler_params=pltpu.CompilerParams(
            collective_id=0, has_side_effects=True, vmem_limit_bytes=VMEM_LIMIT
        ),
    )(hidden, out_grad)


def by_xla(hidden, out_grad):
    spread = lax.all_to_all(out_grad, "fsdp", split_axis=1, concat_axis=0, tiled=True)
    grad_rows = lax.all_gather(spread, "rep", axis=0, tiled=True)
    hidden_rows = lax.all_gather(hidden, ("rep", "fsdp"), axis=0, tiled=True)
    summed = lax.dot_general(
        grad_rows, hidden_rows, (((0,), (0,)), ((), ())), preferred_element_type=jnp.float32
    )
    return summed, jnp.sum(summed * summed)


def kernel_fits(n_rep, n_fsdp, n_tp, rows, columns, features):
    tokens, half = rows * n_rep * n_fsdp, features // n_fsdp
    held_bytes = 2 * (tokens * columns + 2 * tokens * half + half * columns)
    aligned = rows % 16 == 0 and columns % LANES == 0 and half % (LANES * n_tp) == 0
    return n_fsdp == 2 and aligned and half % 256 == 0 and held_bytes < VMEM_LIMIT * 3 // 4


def solution(mesh):
    n_rep, n_fsdp, n_tp = (mesh.shape[axis] for axis in ("rep", "fsdp", "tp"))

    def on_device(gate_pre, up_pre, out_grad):
        hidden = (jax.nn.silu(gate_pre.astype(jnp.float32)) * up_pre.astype(jnp.float32)).astype(
            jnp.bfloat16
        )
        if kernel_fits(n_rep, n_fsdp, n_tp, *hidden.shape, out_grad.shape[1]):
            summed, squares = by_kernel(n_rep, n_tp, hidden, out_grad)
            square_sum = jnp.sum(squares)
        else:
            summed, square_sum = by_xla(hidden, out_grad)
        square_total = lax.psum(square_sum, ("fsdp", "tp"))
        entry_count = summed.shape[0] * n_fsdp * summed.shape[1] * n_tp
        factor = 1.0 / jnp.sqrt(square_total / entry_count + 1e-06)
        return (summed.astype(jnp.float32) * factor).astype(jnp.bfloat16)

    return jax.shard_map(
        on_device,
        mesh=mesh,
        in_specs=(P(("rep", "fsdp"), "tp"), P(("rep", "fsdp"), "tp"), P(("rep", "fsdp"), None)),
        out_specs=P("fsdp", "tp"),
        check_vma=False,
    )
```

time: 309 us -> 142 us (0.46)
  waiting for transfers between devices: 194 us -> 0 us
  Pallas kernels: 0 us -> 107 us
  matrix products: 28.3 us -> 0 us
  local copies, waits for them, and re-layouts: 22 us -> 0 us
  between operations: 14.1 us -> 0.7 us
  blocking collectives: 30.1 us -> 18.4 us
  other arithmetic: 19.4 us -> 15.7 us
    all_gather x2 -> x0, waiting for transfers between devices: 194 us -> none  [the longest x1 115 us: on_device(): hidden_rows = lax.all_gather(hidden, ('rep', 'fsdp'), axis=0, tiled=True)]
    pallas_call x0 -> x1, Pallas kernels: none -> 107 us  [by_kernel(): pl.pallas_call(functools.partial(gather_multiply, n_rep, n_tp), out_shape...]
    dot_general x1 -> x0, matrix products: 28.3 us -> none  [on_device(): lax.dot_general(grad_rows, hidden_rows, (((0,), (0,)), ((), ())), preferr...]
    convert_element_type x1 -> x0, local copies, waits for them, and re-layouts: 19 us -> none  [on_device(): return (summed * factor).astype(jnp.bfloat16)]
    all_to_all x1 -> x0, blocking collectives: 17.6 us -> none  [on_device(): lax.all_to_all(out_grad, 'fsdp', split_axis=1, concat_axis=0, tiled=True)]
    psum x1, blocking collectives: 12.4 us -> 18.4 us  [on_device(): square_total = lax.psum(square_sum, ('fsdp', 'tp'))]
    convert_element_type x1, other arithmetic: 16.7 us -> 11.4 us  [on_device(): return (summed.astype(jnp.float32) * factor).astype(jnp.bfloat16)]
  transfers between devices with their start and end apart: 2 -> 0, of which waited for: 2 -> 0; matrix products, arithmetic and copies ran while one was open for 1% -> 0% of each run, Pallas kernels for 0% -> 0%
where the time goes in v2:
time: 142 us
  Pallas kernels  107 us (75%)
  blocking collectives  18.4 us (13%)
  other arithmetic  15.7 us (11%)
    pallas_call x1, Pallas kernels, by_kernel(): pl.pallas_call(functools.partial(gather_multiply, n_rep, n_tp), out_shape...  107 us
    psum x1, blocking collectives, on_device(): square_total = lax.psum(square_sum, ('fsdp', 'tp'))  18.4 us
    convert_element_type x1, other arithmetic, on_device(): return (summed.astype(jnp.float32) * factor).astype(jnp.bfloat16)  11.4 us
    convert_element_type x1, other arithmetic, on_device(): (jax.nn.silu(gate_pre.astype(jnp.float32)) * up_pre.astype(jnp.float32))....  2.98 us

profile of v2, /device:TPU:0, one launch (start us, length us, event | category | flops | bytes accessed | tf_op | source)
XLA Modules:
  0.0 142.0 jit_solution(10115413176121929788)
XLA Ops:
  0.0 3.0 %fusion.4.hidden_ref = bf16[128,3712]{1,0:T(8,128)(2,1)} fusion(bf16[128,3712]{1,0:T(8,128)(2,1)} %param.4, bf16[128,3712]{1,0:T(8,128)(2,1)} %param.3), kind=kLoop, calls=%fused_computation.7 | loop fusion | flops 3801088 | bytes 2850816 | tf_op jit(solution)/shard_map/convert_element_type | solution.py:314
  3.0 107.2 %shard_map.37 = (bf16[2048,3712]{1,0:T(8,128)(2,1)}, f32[8,128]{1,0:T(8,128)}) custom-call(bf16[128,3712]{1,0:T(8,128)(2,1)} %fusion.4.hidden_ref, bf16[128,4096]{1,0:T(8,128)(2,1)} %grad_ref.1), custom_call_target="tpu_custom_call" | custom-call | tf_op jit(solution)/shard_map/pallas_call | solution.py:267
  110.2 1.3 reduce_sum.9
  111.5 18.4 %psum.7 = f32[]{:T(128)} all-reduce(f32[]{:T(128)} %reduce_sum.9), channel_id=1, replica_groups=mesh['rep'=4,'fsdp'=2,'tp'=4] {'fsdp','tp'}, use_global_device_ids=true, to_apply=%region_1.2 | all-reduce | flops 1 | bytes 8 | tf_op jit(solution)/shard_map/psum | solution.py:322
  130.6 11.4 %multiply_convert_fusion = bf16[2048,3712]{1,0:T(8,128)(2,1)} fusion(bf16[2048,3712]{1,0:T(8,128)(2,1)} %get-tuple-element.7, f32[]{:T(128)S(6)} %sqrt.3), kind=kLoop, calls=%fused_computation | loop fusion | flops 22806528 | bytes 30408708 | tf_op jit(solution)/shard_map/convert_element_type | solution.py:325

commit v3 on v2

--- a/solution.py
+++ b/solution.py
@@ -22,10 +22,10 @@
 
 
 def gather_multiply(
-    n_rep, n_tp, hidden_ref, grad_ref, out_ref, square_ref,
-    held, grads, turned, staged,
+    n_rep, n_tp, entry_count, hidden_ref, grad_ref, out_ref, factor_ref,
+    held, grads, turned, sums,
     local_sem, gx_send, gx_recv, gz_send, gz_recv, gt_send, gt_recv,
-    hz_send, hz_recv, hx_send, hx_recv, out_sem,
+    hz_send, hz_recv, hx_send, hx_recv, sq_send, sq_recv,
 ):
     rep = lax.axis_index("rep")
     fsdp = lax.axis_index("fsdp")
@@ -57,6 +57,10 @@
         pl.semaphore_signal(
             barrier, inc=1, device_id={"tp": lax.rem(tp + k, n_tp)}, device_id_type=MESH
         )
+        pl.semaphore_signal(
+            barrier, inc=1, device_id={"fsdp": 1 - fsdp, "tp": lax.rem(tp + k, n_tp)},
+            device_id_type=MESH,
+        )
     for step in steps:
         @pl.when(within(rep + step))
         def _():
@@ -64,7 +68,7 @@
                 barrier, inc=1, device_id={"rep": rep + step}, device_id_type=MESH
             )
     along = jnp.where(rep > 0, 1, 0) + jnp.where(rep < n_rep - 1, 1, 0)
-    pl.semaphore_wait(barrier, n_tp + along)
+    pl.semaphore_wait(barrier, 2 * n_tp - 1 + along)
 
     def remote(src, dst, send, recv, device):
         return pltpu.make_async_remote_copy(
@@ -194,11 +198,8 @@
         turned[spot, :] = grads[:, spot].T
 
     local_hidden.wait()
-    square_ref[...] = jnp.zeros_like(square_ref)
-
-    def out_copy(c):
-        cols = pl.ds(chunks[c][0], chunks[c][1])
-        return pltpu.make_async_copy(staged.at[:, cols], out_ref.at[:, cols], out_sem.at[c])
+    mine = fsdp * n_tp + tp
+    sums[mine] = jnp.zeros(sums.shape[1:], sums.dtype)
 
     def multiply(c):
         start, size = chunks[c]
@@ -212,14 +213,12 @@
         def _(m):
             spot = pl.ds(pl.multiple_of(m * tile, tile), tile)
             product = jnp.dot(turned[spot, :], held[:, cols], preferred_element_type=jnp.float32)
-            staged[spot, cols] = product.astype(staged.dtype)
+            out_ref[spot, cols] = product.astype(out_ref.dtype)
             squares = jnp.sum((product * product).reshape(tile // 8, 8, size), axis=0)
             total = squares[:, :LANES]
             for at in range(LANES, size, LANES):
                 total = total + squares[:, at:at + LANES]
-            square_ref[...] += total
-
-        out_copy(c).start()
+            sums[mine] += total
 
     for c in range(count):
         for i in range(2):
@@ -253,11 +252,28 @@
                     for c in range(count):
                         hidden_hop(i, d, c).wait_send()
                 if_forwards(i, d, sent_on)
-    for c in range(count):
-        out_copy(c).wait()
-
-
-def by_kernel(n_rep, n_tp, hidden, out_grad):
+
+    peers = [(across_k, k) for across_k in range(2) for k in range(n_tp) if across_k or k]
+
+    def exchange(at, towards):
+        side, k = peers[at]
+        to_side = 1 - fsdp if side else fsdp
+        to_tp = lax.rem(tp + (k if towards else n_tp - k), n_tp)
+        spot = sums.at[mine if towards else to_side * n_tp + to_tp]
+        return remote(spot, spot, sq_send.at[at], sq_recv.at[at], {"fsdp": to_side, "tp": to_tp})
+
+    for at in range(len(peers)):
+        exchange(at, True).start()
+    for at in range(len(peers)):
+        exchange(at, False).wait_recv()
+    square_total = jnp.sum(jnp.sum(sums[...], axis=0), keepdims=True)
+    factor = 1.0 / jnp.sqrt(square_total / entry_count + 1e-06)
+    factor_ref[...] = jnp.broadcast_to(factor, factor_ref.shape)
+    for at in range(len(peers)):
+        exchange(at, True).wait_send()
+
+
+def by_kernel(n_rep, n_tp, entry_count, hidden, out_grad):
     rows, columns = hidden.shape
     tokens = rows * n_rep * 2
     half = out_grad.shape[1] // 2
@@ -265,29 +281,70 @@
     dma = pltpu.SemaphoreType.DMA
     places = 1 + 2 * (n_rep - 1)
     return pl.pallas_call(
-        functools.partial(gather_multiply, n_rep, n_tp),
+        functools.partial(gather_multiply, n_rep, n_tp, entry_count),
         out_shape=(
-            jax.ShapeDtypeStruct((half, columns), jnp.bfloat16),
-            jax.ShapeDtypeStruct((8, LANES), jnp.float32),
+            pltpu.VMEM((half, columns), jnp.bfloat16),
+            pltpu.VMEM((8, LANES), jnp.float32),
         ),
         in_specs=[pl.BlockSpec(memory_space=pl.ANY)] * 2,
-        out_specs=(pl.BlockSpec(memory_space=pl.ANY), pl.BlockSpec(memory_space=pltpu.VMEM)),
+        out_specs=(pl.BlockSpec(memory_space=pltpu.VMEM), pl.BlockSpec(memory_space=pltpu.VMEM)),
         scratch_shapes=[
             pltpu.VMEM((tokens, columns), jnp.bfloat16),
             pltpu.VMEM((tokens, half), jnp.bfloat16),
             pltpu.VMEM((half, tokens), jnp.bfloat16),
-            pltpu.VMEM((half, columns), jnp.bfloat16),
+            pltpu.VMEM((2 * n_tp, 8, LANES), jnp.float32),
             dma((2,)), dma, dma,
             dma((2, n_rep - 1)), dma((2, n_rep - 1)),
             dma((places, n_tp - 1)), dma((places, n_tp - 1)),
             dma((2, n_rep - 1, count)), dma((2, n_rep - 1, count)),
             dma((places, count)), dma((places, count)),
-            dma((count,)),
+            dma((2 * n_tp - 1,)), dma((2 * n_tp - 1,)),
         ],
         compiler_params=pltpu.CompilerParams(
-            collective_id=0, has_side_effects=True, vmem_limit_bytes=VMEM_LIMIT
+            collective_id=0, has_side_effects=True, vmem_limit_bytes=VMEM_LIMIT * 2 // 3
         ),
     )(hidden, out_grad)
+
+
+def scale(summed, factors):
+    half, columns = summed.shape
+    rows = 128
+
+    def body(summed_ref, factor_ref, out_ref, ready, sems):
+        steps = half // rows
+        depth = ready.shape[0]
+
+        def leave(m):
+            slot = lax.rem(m, depth)
+            spot = pl.ds(pl.multiple_of(m * rows, rows), rows)
+            return pltpu.make_async_copy(ready.at[slot], out_ref.at[spot, :], sems.at[slot])
+
+        @pl.loop(0, steps)
+        def _(m):
+            slot = lax.rem(m, depth)
+            spot = pl.ds(pl.multiple_of(m * rows, rows), rows)
+
+            @pl.when(m >= depth)
+            def _():
+                leave(m - depth).wait()
+            for at in range(0, columns, LANES):
+                cols = pl.ds(at, LANES)
+                scaled = summed_ref[spot, cols].astype(jnp.float32) * factor_ref[0:1, :]
+                ready[slot, :, cols] = scaled.astype(ready.dtype)
+            leave(m).start()
+
+        @pl.loop(max(steps - depth, 0), steps)
+        def _(m):
+            leave(m).wait()
+
+    return pl.pallas_call(
+        body,
+        out_shape=jax.ShapeDtypeStruct((half, columns), jnp.bfloat16),
+        in_specs=[pl.BlockSpec(memory_space=pltpu.VMEM)] * 2,
+        out_specs=pl.BlockSpec(memory_space=pl.ANY),
+        scratch_shapes=[pltpu.VMEM((4, rows, columns), jnp.bfloat16), pltpu.SemaphoreType.DMA((4,))],
+        compiler_params=pltpu.CompilerParams(vmem_limit_bytes=16 * 1024 * 1024),
+    )(summed, factors)
 
 
 def by_xla(hidden, out_grad):
@@ -314,15 +371,15 @@
         hidden = (jax.nn.silu(gate_pre.astype(jnp.float32)) * up_pre.astype(jnp.float32)).astype(
             jnp.bfloat16
         )
+        half, columns = out_grad.shape[1] // n_fsdp, hidden.shape[1]
+        entry_count = half * n_fsdp * columns * n_tp
         if kernel_fits(n_rep, n_fsdp, n_tp, *hidden.shape, out_grad.shape[1]):
-            summed, squares = by_kernel(n_rep, n_tp, hidden, out_grad)
-            square_sum = jnp.sum(squares)
-        else:
-            summed, square_sum = by_xla(hidden, out_grad)
+            summed, factors = by_kernel(n_rep, n_tp, entry_count, hidden, out_grad)
+            return scale(summed, factors)
+        summed, square_sum = by_xla(hidden, out_grad)
         square_total = lax.psum(square_sum, ("fsdp", "tp"))
-        entry_count = summed.shape[0] * n_fsdp * summed.shape[1] * n_tp
         factor = 1.0 / jnp.sqrt(square_total / entry_count + 1e-06)
-        return (summed.astype(jnp.float32) * factor).astype(jnp.bfloat16)
+        return (summed * factor).astype(jnp.bfloat16)
 
     return jax.shard_map(
         on_device,

time: 142 us -> 122 us (0.86)
  blocking collectives: 18.4 us -> 0 us
  other arithmetic: 15.7 us -> 2.98 us
  Pallas kernels: 107 us -> 119 us
    psum x1 -> x0, blocking collectives: 18.4 us -> none  [on_device(): square_total = lax.psum(square_sum, ('fsdp', 'tp'))]
    pallas_call x1 -> x2, Pallas kernels: 107 us -> 119 us  [the longest x1 113 us: by_kernel(): pl.pallas_call(functools.partial(gather_multiply, n_rep, n_tp, entry_coun...]
    convert_element_type x1 -> x0, other arithmetic: 11.4 us -> none  [on_device(): return (summed.astype(jnp.float32) * factor).astype(jnp.bfloat16)]
where the time goes in v3:
time: 122 us
  Pallas kernels  119 us (98%)
  other arithmetic  2.98 us (2%)
    pallas_call x1, Pallas kernels, by_kernel(): pl.pallas_call(functools.partial(gather_multiply, n_rep, n_tp, entry_coun...  113 us
    pallas_call x1, Pallas kernels, scale(): pl.pallas_call(body, out_shape=jax.ShapeDtypeStruct((half, columns), jnp....  5.58 us
    convert_element_type x1, other arithmetic, on_device(): (jax.nn.silu(gate_pre.astype(jnp.float32)) * up_pre.astype(jnp.float32))....  2.98 us

profile of v3, /device:TPU:0, one launch (start us, length us, event | category | flops | bytes accessed | tf_op | source)
XLA Modules:
  0.0 122.0 jit_solution(2660433441792268322)
XLA Ops:
  0.0 3.0 %fusion.4.hidden_ref = bf16[128,3712]{1,0:T(8,128)(2,1)} fusion(bf16[128,3712]{1,0:T(8,128)(2,1)} %param.4, bf16[128,3712]{1,0:T(8,128)(2,1)} %param.3), kind=kLoop, calls=%fused_computation.6 | loop fusion | flops 3801088 | bytes 2850816 | tf_op jit(solution)/shard_map/convert_element_type | solution.py:371
  3.0 113.5 %shard_map.37 = (bf16[2048,3712]{1,0:T(8,128)(2,1)S(1)}, f32[8,128]{1,0:T(8,128)S(1)}) custom-call(bf16[128,3712]{1,0:T(8,128)(2,1)} %fusion.4.hidden_ref, bf16[128,4096]{1,0:T(8,128)(2,1)} %grad_ref.1), custom_call_target="tpu_custom_call" | custom-call | tf_op jit(solution)/shard_map/pallas_call | solution.py:283
  116.5 5.6 %shard_map.38 = bf16[2048,3712]{1,0:T(8,128)(2,1)} custom-call(bf16[2048,3712]{1,0:T(8,128)(2,1)S(1)} %get-tuple-element.7.summed_ref, f32[8,128]{1,0:T(8,128)S(1)} %get-tuple-element.8.factor_ref), custom_call_target="tpu_custom_call" | custom-call | tf_op jit(solution)/shard_map/pallas_call | solution.py:340
